TPU v7x, 32 devices: a whole 2x2x4 slice. The times are simulated.
32 devices in a mesh: dp: 4 (over z), neg: 8 (over y, x, core).
Axes of the slice: x: 2, y: 2, z: 4, core: 2. Of those that a mesh axis runs over, the one named last changes fastest.
Arguments:
- query_emb: bfloat16 [128, 32, 128], P(('dp', 'neg')), may hold values from -6 to 6
- positive: int32 [128], P(('dp', 'neg')), may hold values from 0 to 31
- passage_emb: bfloat16 [32, 512, 128], P(('dp', 'neg')), may hold values from -6 to 6
- lengths: int32 [32], P(('dp', 'neg')), may hold values from 256 to 512
- residual: bfloat16 [16384, 1024], P(('dp', 'neg')), may hold values from -6 to 6
- context: bfloat16 [16384, 1024], P(('dp', 'neg')), may hold values from -6 to 6
- out_proj: bfloat16 [1024, 1024], replicated, may hold values from -0.1875 to 0.1875
- norm_gain: float32 [1024], replicated, may hold values from 0.5 to 1.5
- colbert_proj: bfloat16 [1024, 128], replicated, may hold values from -0.1875 to 0.1875
Outputs:
- loss: float32 [], replicated
- query_grad: float32 [128, 32, 128], P(('dp', 'neg'))
- residual_grad: bfloat16 [16384, 1024], P(('dp', 'neg'))
- context_grad: bfloat16 [16384, 1024], P(('dp', 'neg'))
- out_proj_grad: float32 [1024, 1024], replicated
- colbert_grad: float32 [1024, 128], replicated
- gain_grad: float32 [1024], replicated
Inputs may be any that keep to these rules, and one draw needn't show every extreme that they name: A passage's first lengths[p] token slots are real, the rest padding.
All inputs are finite; a program needn't handle non-finite values.
Results may differ from a plain program's by a relative error of at most 0.0065.
Values may be sent and summed in bfloat16 or wider, within the bound.
A program may use at most 64 MiB of HBM per device.

v0:
```python
import math

import jax
import jax.numpy as jnp
from jax import lax
from jax.sharding import PartitionSpec as P


def combined_all(array, axis, combine):
    everything = jax.tree.map(lambda part: lax.all_gather(part, axis), array)
    initial = jax.tree.map(lambda part: part[0], everything)

    def turn(k, so_far):
        return combine(so_far, jax.tree.map(lambda part: part[k], everything))

    return lax.fori_loop(1, lax.axis_size(axis), turn, initial)


def block_plan(query_count, query_len):
    return math.gcd(query_count, max(1, 2048 // query_len))


def masked_scores(query_block, passage_one, usable):
    scores = jnp.einsum("rd,jd->rj", query_block, passage_one, preferred_element_type=jnp.float32)
    return jnp.where(usable, scores, -1e30)


def tile_forward(query_tokens, query_pos, passage_tokens, passage_len, passage_ids):
    query_count, query_len, emb_width = query_tokens.shape
    per_block = block_plan(query_count, query_len)
    query_blocks = query_tokens.reshape(query_count // per_block, per_block * query_len, emb_width)

    def per_passage(inputs):
        passage_one, length = inputs
        usable = (jnp.arange(passage_one.shape[0]) < length)[None, :]

        def per_query(query_block):
            masked = masked_scores(query_block, passage_one, usable)
            highest = jnp.max(masked, axis=1, keepdims=True)
            return highest[:, 0] + jnp.log(jnp.sum(jnp.exp(masked - highest), axis=1))

        inner_lse = lax.map(per_query, query_blocks).reshape(query_count, query_len)
        shifted = inner_lse - jnp.log(length.astype(jnp.float32))
        return (inner_lse, jnp.sum(shifted, axis=1))

    inner_all, similar = lax.map(per_passage, (passage_tokens, passage_len))
    similar = similar.T
    is_positive = passage_ids[None, :] == query_pos[:, None]
    highest = jnp.max(similar, axis=1)
    exp_total = jnp.sum(jnp.exp(similar - highest[:, None]), axis=1)
    positive_score = jnp.sum(jnp.where(is_positive, similar, 0.0), axis=1)
    return (inner_all, similar, is_positive, (highest, exp_total, positive_score))


def combine_totals(earlier, later):
    highest = jnp.maximum(earlier[0], later[0])
    exp_total = earlier[1] * jnp.exp(earlier[0] - highest) + later[1] * jnp.exp(later[0] - highest)
    return (highest, exp_total, earlier[2] + later[2])


def finish_rows(similar, is_positive, totals, own_block, query_dev):
    log_total = totals[0] + jnp.log(totals[1])
    coefficient = jnp.exp(similar - log_total[:, None]) - is_positive.astype(jnp.float32)
    own_terms = lax.dynamic_slice_in_dim(log_total - totals[2], own_block * query_dev, query_dev)
    return (coefficient, jnp.sum(own_terms))


def tile_backward(query_tokens, passage_tokens, passage_len, inner_all, coefficient):
    query_count, query_len, emb_width = query_tokens.shape
    per_block = block_plan(query_count, query_len)
    block_count = query_count // per_block
    query_blocks = query_tokens.reshape(block_count, per_block * query_len, emb_width)

    def per_passage(running, inputs):
        passage_one, length, inner_lse, column = inputs
        usable = (jnp.arange(passage_one.shape[0]) < length)[None, :]

        def per_query(pieces):
            query_block, inner_block, column_block = pieces
            masked = masked_scores(query_block, passage_one, usable)
            spread = jnp.exp(masked - inner_block.reshape(-1)[:, None]).reshape(
                per_block, query_len, -1
            )
            weight = (
                (spread * column_block[:, None, None])
                .reshape(per_block * query_len, -1)
                .astype(jnp.bfloat16)
            )
            query_part = jnp.dot(weight, passage_one, preferred_element_type=jnp.float32)
            passage_part = jnp.einsum(
                "rj,rd->jd", weight, query_block, preferred_element_type=jnp.float32
            )
            return (query_part, passage_part)

        query_parts, passage_parts = lax.map(
            per_query,
            (
                query_blocks,
                inner_lse.reshape(block_count, per_block, query_len),
                column.reshape(block_count, per_block),
            ),
        )
        return (running + query_parts.reshape(running.shape), jnp.sum(passage_parts, axis=0))

    start = jnp.zeros((query_count * query_len, emb_width), jnp.float32)
    query_sum, passage_sum = lax.scan(
        per_passage, start, (passage_tokens, passage_len, inner_all, coefficient.T)
    )
    return (query_sum.reshape(query_count, query_len, emb_width), passage_sum)


def window_rows(resid_rows, context_rows, grad_rows, out_proj, norm_gain, colbert_proj):
    hidden = resid_rows.astype(jnp.float32) + jnp.dot(
        context_rows, out_proj, preferred_element_type=jnp.float32
    )
    row_mean = jnp.mean(hidden, axis=1, keepdims=True)
    centred = hidden - row_mean
    variance = jnp.mean(centred * centred, axis=1, keepdims=True)
    inv_std = 1.0 / jnp.sqrt(variance + 1e-05)
    normed = centred * inv_std
    scaled = (normed * norm_gain).astype(jnp.bfloat16)
    colbert_part = jnp.dot(scaled.T, grad_rows, preferred_element_type=jnp.float32)
    scaled_grad = jnp.dot(grad_rows, colbert_proj.T, preferred_element_type=jnp.float32)
    gain_part = jnp.sum(scaled_grad * normed, axis=0)
    gained = scaled_grad * norm_gain
    hidden_grad = (
        inv_std
        * (
            gained
            - jnp.mean(gained, axis=1, keepdims=True)
            - normed * jnp.mean(gained * normed, axis=1, keepdims=True)
        )
    ).astype(jnp.bfloat16)
    context_grad = jnp.dot(hidden_grad, out_proj.T, preferred_element_type=jnp.float32).astype(
        jnp.bfloat16
    )
    proj_part = jnp.dot(context_rows.T, hidden_grad, preferred_element_type=jnp.float32)
    return (hidden_grad, context_grad, proj_part, colbert_part, gain_part)


def body(
    query_emb, positive, passage_emb, lengths, residual, context, out_proj, norm_gain, colbert_proj
):
    query_dev = query_emb.shape[0]
    passage_dev = passage_emb.shape[0]
    neg_size = lax.axis_size("neg")
    neg_place = lax.axis_index("neg")
    query_tokens, query_pos = (
        lax.all_gather(query_emb, "neg", axis=0, tiled=True),
        lax.all_gather(positive, "neg", axis=0, tiled=True),
    )
    passage_tokens, passage_len = (
        lax.all_gather(passage_emb, "dp", axis=0, tiled=True),
        lax.all_gather(lengths, "dp", axis=0, tiled=True),
    )
    position = jnp.arange(passage_tokens.shape[0], dtype=jnp.int32)
    passage_ids = (
        position // passage_dev * neg_size + neg_place
    ) * passage_dev + position % passage_dev
    inner_all, similar, is_positive, stats = tile_forward(
        query_tokens, query_pos, passage_tokens, passage_len, passage_ids
    )
    totals = combined_all(stats, "neg", combine_totals)
    coefficient, loss_part = finish_rows(similar, is_positive, totals, neg_place, query_dev)
    query_sum, passage_sum = tile_backward(
        query_tokens, passage_tokens, passage_len, inner_all, coefficient
    )
    query_grad = lax.psum_scatter(query_sum, "neg", scatter_dimension=0, tiled=True)
    emb_sum = lax.psum_scatter(passage_sum, "dp", scatter_dimension=0, tiled=True)
    emb_grad = emb_sum.astype(jnp.bfloat16).reshape(
        passage_dev * emb_sum.shape[1], emb_sum.shape[2]
    )
    residual_grad, context_grad, proj_part, colbert_part, gain_part = window_rows(
        residual, context, emb_grad, out_proj, norm_gain, colbert_proj
    )
    out_proj_grad, colbert_grad, gain_grad, loss_total = lax.psum(
        (proj_part, colbert_part, gain_part, loss_part), ("dp", "neg")
    )
    loss = loss_total / (query_dev * lax.axis_size("dp") * neg_size)
    return (loss, query_grad, residual_grad, context_grad, out_proj_grad, colbert_grad, gain_grad)


def solution(mesh):
    in_specs = (
        P(("dp", "neg"), None, None),
        P(("dp", "neg")),
        P(("dp", "neg"), None, None),
        P(("dp", "neg")),
        P(("dp", "neg"), None),
        P(("dp", "neg"), None),
        P(),
        P(),
        P(),
    )
    out_specs = (
        P(),
        P(("dp", "neg"), None, None),
        P(("dp", "neg"), None),
        P(("dp", "neg"), None),
        P(),
        P(),
        P(),
    )
    return jax.shard_map(body, mesh=mesh, in_specs=in_specs, out_specs=out_specs, check_vma=False)
```

profile of v0, /device:TPU:29, one launch (start us, length us, event | category | flops | bytes accessed | tf_op | source)
XLA Modules:
  0.0 299.8 jit_solution(8071022490365719969)
XLA Ops:
  8.9 1.2 dynamic-slice
  10.9 4.2 %all-reduce = s32[4]{0:T(128)S(1)} all-reduce(s32[4]{0:T(128)S(1)} %dynamic-update-slice), channel_id=1, replica_groups=mesh['dp'=4,'neg'=8] {'dp'}, use_global_device_ids=true, to_apply=%add | all-reduce | flops 4 | bytes 32
  15.1 15.4 %all_gather.31 = bf16[4,512,128]{2,1,0:T(8,128)(2,1)} all-gather(bf16[1,512,128]{2,1,0:T(8,128)(2,1)} %param.17), channel_id=1, replica_groups=mesh['dp'=4,'neg'=8] {'dp'}, dimensions={0}, use_global_device_ids=true | all-gather | bytes 655360 | tf_op jit(solution)/shard_map/all_gather | solution.py:153
  30.5 13.7 %all_gather.32 = bf16[32,32,128]{2,1,0:T(8,128)(2,1)S(1)} all-gather(bf16[4,32,128]{2,1,0:T(8,128)(2,1)} %param.15), channel_id=1, replica_groups=mesh['dp'=4,'neg'=8] {'neg'}, dimensions={0}, use_global_device_ids=true | all-gather | bytes 294912 | tf_op jit(solution)/shard_map/all_gather | solution.py:149
  44.2 16.2 %while.53 = (s32[]{:T(128)}, f32[4,32,32]{2,1,0:T(8,128)S(1)}, f32[4,32]{1,0:T(4,128)S(1)}, s32[4]{0:T(128)S(1)}, bf16[4,512,128]{2,1,0:T(8,128)(2,1)}, /*index=...) while((s32[]{:T(128)}, f32[4,32,32]{2,1,0:T(8,128)S(1)}, f32[4,32]{1,0:T(4,128)S(1)}, ...), condition=%wide.region_4.5_spmd, body=%wide.region_0.4_spmd.sunk | while | flops 136840672 | bytes 4672013 | solution.py:46
  45.4 1.4 select_reduce_fusion.2
  49.5 1.4 select_reduce_fusion.2
  53.5 1.4 select_reduce_fusion.2
  57.6 1.4 select_reduce_fusion.2
  61.9 5.3 %all-reduce.3 = s32[32]{0:T(128)S(1)} all-reduce(s32[32]{0:T(128)S(1)} %dynamic-update-slice.3), channel_id=1, replica_groups=mesh['dp'=4,'neg'=8] {'neg'}, use_global_device_ids=true, to_apply=%add.3 | all-reduce | flops 32 | bytes 256
  68.6 13.0 %all-reduce.7 = (f32[256]{0:T(256)S(1)}, f32[256]{0:T(256)S(1)}, f32[256]{0:T(256)S(1)}) all-reduce(f32[256]{0:T(256)S(1)} %dynamic-update-slice.1, f32[256]{0:T(256)S(1)} %dynamic-update-slice.2, f32[256]{0:T(256)S(1)} %dynamic-update-slice.4), channel_id=2, replica_groups=mesh['dp'=4,'neg'=8] {'neg'}, use_global_device_ids=true, to_apply=%add.1 | all-reduce | flops 768 | bytes 6144
  82.3 25.8 %while.55 = (s32[]{:T(128)}, f32[1024,128]{1,0:T(8,128)}, f32[4,512,128]{2,1,0:T(8,128)}, s32[4]{0:T(128)S(1)}, bf16[4,512,128]{2,1,0:T(8,128)(2,1)}, /*index=5*...) while((s32[]{:T(128)}, f32[1024,128]{1,0:T(8,128)}, ...), condition=%wide.region_13.14_spmd.clone, body=%wide.region_12.13_spmd.clone.sunk | while | flops 405012992 | bytes 5282823 | solution.py:106
  83.7 1.5 multiply_convert_fusion.5
  85.2 1.2 fusion.63
  86.4 2.2 convolution_add_fusion.2
  90.0 1.5 multiply_convert_fusion.5
  91.5 1.2 fusion.63
  92.7 2.4 convolution_add_fusion.2
  96.5 1.5 multiply_convert_fusion.5
  99.2 2.4 convolution_add_fusion.2
  103.0 1.5 multiply_convert_fusion.5
  105.7 2.4 convolution_add_fusion.2
  108.1 2.9 fusion.36
  111.0 1.3 copy-done.1
  112.7 19.9 %reduce-scatter.5.cloned.1.call-done = f32[1,512,128]{2,1,0:T(8,128)} async-done(((f32[4,512,128]{2,1,0:T(8,128)}), f32[1,512,128]{2,1,0:T(8,128)}) %reduce-scatter.5.cloned.1.call-update) | async-done | bytes 262160 | tf_op jit(solution)/shard_map/reduce_scatter | solution.py:169
  132.6 2.7 multiply_reduce_fusion
  136.5 3.3 %convolution_bitcast_fusion.1 = f32[1024,1024]{0,1:T(8,128)} fusion(bf16[512,1024]{1,0:T(8,128)(2,1)S(1)} %multiply_convert_fusion.2, bf16[512,1024]{1,0:T(8,128)(2,1)S(1)} %copy-done.5), kind=kOutput, calls=%fused_computation.37 | convolution fusion | flops 1073741824 | bytes 6291456 | tf_op jit(solution)/shard_map/dot_general | solution.py:137
  139.8 1.6 fusion.22
  142.7 40.7 %all-reduce.5 = (f32[]{:T(128)}, f32[1024]{0:T(1024)}) all-reduce(f32[]{:T(128)} %dynamic-slice_reduce_fusion, f32[1024]{0:T(1024)S(1)} %get-tuple-element.355), channel_id=1, replica_groups=mesh['dp'=4,'neg'=8] {'dp','neg'}, use_global_device_ids=true, to_apply=%region_11.12 | all-reduce | flops 1025 | bytes 8200 | tf_op jit(solution)/shard_map/psum | solution.py:176
  184.1 2.3 convolution_convert_fusion
  186.3 98.7 %all-reduce.10.cloned.1.call-done = (f32[1024,1024]{0,1:T(8,128)}, f32[1024,128]{1,0:T(8,128)}) async-done(((f32[1024,1024]{0,1:T(8,128)}, f32[1024,128]{1,0:T(8,128)}), (f32[1024,1024]{0,1:T(8,128)}, f32[1024,128]{1,0:T(8,128)})) %all-reduce.10.cloned.1.call-update) | async-done | bytes 4718608 | tf_op jit(solution)/shard_map/psum | solution.py:176
  285.0 5.4 %copy.18 = f32[1024,1024]{1,0:T(8,128)} copy(f32[1024,1024]{0,1:T(8,128)} %get-tuple-element.404) | data formatting | bytes 8388608
  (135 shorter events, 23.0 us)
Async XLA Ops:
  8.0 100.1 %copy-start = (bf16[1024,1024]{1,0:T(8,128)(2,1)S(1)}, bf16[1024,1024]{1,0:T(8,128)(2,1)}, u32[]{:S(2)}) copy-start(bf16[1024,1024]{1,0:T(8,128)(2,1)} %param.21) | copy-start | bytes 6291460
  8.0 124.5 %reduce-scatter.5.cloned.1.call-start = ((), (), s32[]{:S(2)}) async-start(), calls=%async_computation.3 | async-start | bytes 1310720 | tf_op jit(solution)/shard_map/reduce_scatter | solution.py:169
  44.2 16.2 %copy-start.10 = (u32[32]{0:T(128)S(1)}, u32[32]{0:T(128)}, u32[]{:S(2)}) copy-start(u32[32]{0:T(128)} %constant.164) | copy-start | bytes 388
  44.2 17.5 %copy-start.9 = (s32[4]{0:T(128)S(1)}, s32[4]{0:T(128)}, u32[]{:S(2)}) copy-start(s32[4]{0:T(128)} %param.16) | copy-start | bytes 52
  108.1 177.0 %all-reduce.10.cloned.1.call-start = ((), (), s32[]{:S(2)}) async-start(), calls=%async_computation.4 | async-start | bytes 9437184 | tf_op jit(solution)/shard_map/psum | solution.py:176
  111.0 1.3 copy-start.1
  111.0 21.5 %copy-start.7 = (bf16[1024,128]{1,0:T(8,128)(2,1)S(1)}, bf16[1024,128]{1,0:T(8,128)(2,1)}, u32[]{:S(2)}) copy-start(bf16[1024,128]{1,0:T(8,128)(2,1)} %param.23) | copy-start | bytes 786436
  111.0 21.5 %copy-start.8 = (f32[1024]{0:T(1024)S(1)}, f32[1024]{0:T(1024)}, u32[]{:S(2)}) copy-start(f32[1024]{0:T(1024)} %param.22) | copy-start | bytes 12292
  132.5 2.7 copy-start.2
  135.3 1.2 copy-start.5
  136.5 47.6 %copy-start.3 = (bf16[512,1024]{1,0:T(8,128)(2,1)}, bf16[512,1024]{1,0:T(8,128)(2,1)S(1)}, u32[]{:S(2)}) copy-start(bf16[512,1024]{1,0:T(8,128)(2,1)S(1)} %multiply_convert_fusion.2) | copy-start | bytes 3145732
  136.5 3.3 %copy-start.4 = (f32[1,512,128]{2,1,0:T(8,128)S(1)}, f32[1,512,128]{2,1,0:T(8,128)}, u32[]{:S(2)}) copy-start(f32[1,512,128]{2,1,0:T(8,128)} %reduce-scatter.5.cloned.1.call-done) | copy-start | bytes 786436
  141.4 149.0 %reduce-scatter.3.cloned.1.call-start = ((), (), s32[]{:S(2)}) async-start(), calls=%async_computation.2 | async-start | bytes 589824 | tf_op jit(solution)/shard_map/reduce_scatter | solution.py:168
  285.0 5.4 %copy-start.6 = (f32[1024,128]{1,0:T(8,128)S(1)}, f32[1024,128]{1,0:T(8,128)}, u32[]{:S(2)}) copy-start(f32[1024,128]{1,0:T(8,128)} %get-tuple-element.658) | copy-start | bytes 1572868
Sparse Core Ops, SparseCore 0:
  108.2 24.3 reduce-scatter.4
  141.6 143.4 all-reduce.9
Sparse Core Ops, SparseCore 1:
  145.6 35.1 reduce-scatter.2
where the time goes:
time: 306 us; the launch traced here: 300 us
  waiting for transfers between devices  119 us (39%)
  blocking collectives  92.3 us (30%)
  matrix products  38 us (12%)
  between operations  19.5 us (6%)
  local copies, waits for them, and re-layouts  18.2 us (6%)
  other arithmetic  9.43 us (3%)
  loops' own time  3.08 us (1%)
    psum x1, waiting for transfers between devices, body(): lax.psum((proj_part, colbert_part, gain_part, loss_part), ('dp', 'neg'))  98.7 us
    psum x1, blocking collectives, body(): lax.psum((proj_part, colbert_part, gain_part, loss_part), ('dp', 'neg'))  40.7 us
    unnamed x3, blocking collectives  22.5 us
    reduce_scatter x1, waiting for transfers between devices, body(): lax.psum_scatter(passage_sum, 'dp', scatter_dimension=0, tiled=True)  19.9 us
    all_gather x1, blocking collectives, body(): lax.all_gather(passage_emb, 'dp', axis=0, tiled=True)  15.4 us
    all_gather x1, blocking collectives, body(): lax.all_gather(query_emb, 'neg', axis=0, tiled=True)  13.7 us
    unnamed x36, local copies, waits for them, and re-layouts  11.6 us
    dot_general x8, matrix products, masked_scores(): jnp.einsum('rd,jd->rj', query_block, passage_one, preferred_element_type=...  11.3 us
  transfers between devices with their start and end apart: 3, of which 2 were waited for; matrix products, arithmetic and copies ran while one was open for 4% of the time, Pallas kernels for 0%

commit v1 on v0

v1 whole, which is shorter than its diff:
```python
import functools

import jax
import jax.numpy as jnp
from jax import lax
from jax.experimental import pallas as pl
from jax.experimental.pallas import tpu as pltpu
from jax.sharding import PartitionSpec as P

MESH = pl.DeviceIdType.MESH
VMEM = pl.BlockSpec(memory_space=pltpu.VMEM)
LANES = 128
LOW = -1e30


def place(axis, size, step):
    there = lax.rem(lax.axis_index(axis) + step + size, size)
    if axis == "dp":
        return (there, lax.axis_index("neg"))
    return (lax.axis_index("dp"), there)


def greet(sizes):
    barrier = pltpu.get_barrier_semaphore()
    for axis, size in sizes:

        def tell(k, carry):
            pl.semaphore_signal(
                barrier, inc=1, device_id=place(axis, size, k), device_id_type=MESH
            )
            return carry

        lax.fori_loop(1, size, tell, 0)
    pl.semaphore_wait(barrier, sum(size - 1 for _, size in sizes))


def remote(src, dst, send, recv, device):
    return pltpu.make_async_remote_copy(
        src_ref=src, dst_ref=dst, send_sem=send, recv_sem=recv, device_id=device, device_id_type=MESH
    )


def each(size, act):
    def turn(k, carry):
        act(k)
        return carry

    lax.fori_loop(1, size, turn, 0)


def gather_kernel(sizes, plan, *refs):
    count = len(plan)
    ins, outs, sems = refs[:count], refs[count : 2 * count], refs[2 * count :]
    greet([(axis, sizes[axis]) for axis in dict.fromkeys(plan)])
    for i, axis in enumerate(plan):
        me = lax.axis_index(axis)
        each(
            sizes[axis],
            lambda k: remote(
                ins[i], outs[i].at[me], sems[2 * i].at[k], sems[2 * i + 1].at[k], place(axis, sizes[axis], k)
            ).start(),
        )
    for i, axis in enumerate(plan):
        outs[i][lax.axis_index(axis)] = ins[i][...]
    for i, axis in enumerate(plan):
        size = sizes[axis]
        me = lax.axis_index(axis)

        def finish(k):
            slot = lax.rem(me - k + size, size)
            copy = remote(
                ins[i], outs[i].at[slot], sems[2 * i].at[k], sems[2 * i + 1].at[k], place(axis, size, k)
            )
            copy.wait_recv()
            copy.wait_send()

        each(size, finish)


def gather(sizes, ident, pairs):
    plan = tuple(axis for _, axis in pairs)
    arrays = [array for array, _ in pairs]
    sems = []
    for axis in plan:
        sems += [pltpu.SemaphoreType.DMA((sizes[axis],))] * 2
    return pl.pallas_call(
        functools.partial(gather_kernel, sizes, plan),
        out_shape=[
            jax.ShapeDtypeStruct((sizes[axis],) + array.shape, array.dtype) for array, axis in pairs
        ],
        in_specs=[VMEM] * len(plan),
        out_specs=[VMEM] * len(plan),
        scratch_shapes=sems,
        compiler_params=pltpu.CompilerParams(collective_id=ident, has_side_effects=True),
    )(*arrays)


def scatter_kernel(sizes, plan, *refs):
    count = len(plan)
    ins, outs, rest = refs[:count], refs[count : 2 * count], refs[2 * count :]
    lands, sems = rest[:count], rest[count:]
    greet([(axis, sizes[axis]) for axis in plan])
    for i, axis in enumerate(plan):
        size = sizes[axis]
        me = lax.axis_index(axis)

        each(
            size,
            lambda k: remote(
                ins[i].at[lax.rem(me + k, size)],
                lands[i].at[k],
                sems[2 * i].at[k],
                sems[2 * i + 1].at[k],
                place(axis, size, k),
            ).start(),
        )
    for i, axis in enumerate(plan):
        size = sizes[axis]
        me = lax.axis_index(axis)

        def finish(k):
            copy = remote(
                ins[i].at[lax.rem(me + k, size)],
                lands[i].at[k],
                sems[2 * i].at[k],
                sems[2 * i + 1].at[k],
                place(axis, size, k),
            )
            copy.wait_recv()
            copy.wait_send()

        each(size, finish)
        total = ins[i][me].astype(jnp.float32)
        for k in range(1, size):
            total = total + lands[i][k].astype(jnp.float32)
        outs[i][...] = total.astype(outs[i].dtype)


def scatter(sizes, ident, triples):
    plan = tuple(axis for _, axis, _ in triples)
    sems, lands = [], []
    for array, axis, _ in triples:
        lands.append(pltpu.VMEM(array.shape, array.dtype))
        sems += [pltpu.SemaphoreType.DMA((sizes[axis],))] * 2
    return pl.pallas_call(
        functools.partial(scatter_kernel, sizes, plan),
        out_shape=[jax.ShapeDtypeStruct(array.shape[1:], dtype) for array, _, dtype in triples],
        in_specs=[VMEM] * len(plan),
        out_specs=[VMEM] * len(plan),
        scratch_shapes=lands + sems,
        compiler_params=pltpu.CompilerParams(collective_id=ident, has_side_effects=True),
    )(*[array for array, _, _ in triples])


def total_kernel(dp, neg, part, gain, extra, out, small, pair_in, held, lands, mine, pair_small, all_small,
                 pair_s, pair_r, rs_s, rs_r, ag_s, ag_r, fw_s, fw_r, sm_s, sm_r, sp_s, sp_r):
    groups = neg // 2
    n = dp * groups
    row, col = lax.axis_index("dp"), lax.axis_index("neg")
    core = lax.rem(col, 2)
    other = 1 - core
    me = row * groups + col // 2
    partner = (row, col + 1 - 2 * core)

    def at(k):
        return lax.rem(me + k + n, n)

    def device(k):
        t = at(k)
        return (t // groups, lax.rem(t, groups) * 2 + core)

    barrier = pltpu.get_barrier_semaphore()
    pl.semaphore_signal(barrier, inc=1, device_id=partner, device_id_type=MESH)
    each(n, lambda k: pl.semaphore_signal(barrier, inc=1, device_id=device(k), device_id_type=MESH))
    pl.semaphore_wait(barrier, n)

    wide = gain.shape[1]
    mine[:, :wide] = gain[...]
    mine[:, wide:] = extra[...]

    def pair_copy(k):
        return remote(part.at[other, at(k)], pair_in.at[at(k)], pair_s.at[k], pair_r.at[k], partner)

    def rs_copy(k):
        return remote(held.at[at(k)], lands.at[k], rs_s.at[k], rs_r.at[k], device(k))

    each(n, lambda k: pair_copy(k).start())
    pair_copy(0).start()
    sp_copy = remote(mine, pair_small, sp_s, sp_r, partner)
    sp_copy.start()

    def join(k):
        pair_copy(k).wait_recv()
        t = at(k)
        held[t] = (part[core, t].astype(jnp.float32) + pair_in[t].astype(jnp.float32)).astype(held.dtype)

    def join_send(k):
        join(k)
        rs_copy(k).start()

    each(n, join_send)
    join(0)
    sp_copy.wait_recv()
    all_small[me] = mine[...] + pair_small[...]

    def sm_copy(k, slot):
        return remote(all_small.at[slot], all_small.at[slot], sm_s.at[k], sm_r.at[k], device(k))

    each(n, lambda k: sm_copy(k, me).start())

    def add(k, total):
        rs_copy(k).wait_recv()
        return total + lands[k].astype(jnp.float32)

    total = lax.fori_loop(1, n, add, held[me].astype(jnp.float32))
    out[core, me] = total.astype(out.dtype)

    def ag_copy(k, slot):
        return remote(out.at[core, slot], out.at[core, slot], ag_s.at[k], ag_r.at[k], device(k))

    def fw_copy(k, half):
        return remote(out.at[half, at(-k)], out.at[half, at(-k)], fw_s.at[k], fw_r.at[k], partner)

    each(n, lambda k: ag_copy(k, me).start())
    fw_copy(0, core).start()

    def pass_on(k):
        ag_copy(k, at(-k)).wait_recv()
        fw_copy(k, core).start()

    each(n, pass_on)
    each(n, lambda k: sm_copy(k, at(-k)).wait_recv())

    def add_small(k, so_far):
        return so_far + all_small[k]

    small[...] = lax.fori_loop(1, n, add_small, all_small[0])

    def drain(k):
        fw_copy(k, other).wait_recv()
        fw_copy(k, core).wait_send()
        pair_copy(k).wait_send()

    drain(0)
    sp_copy.wait_send()

    def drain_all(k):
        drain(k)
        rs_copy(k).wait_send()
        ag_copy(k, me).wait_send()
        sm_copy(k, me).wait_send()

    each(n, drain_all)


def total_sum(sizes, ident, part, gain, extra):
    dp, neg = sizes["dp"], sizes["neg"]
    n = dp * neg // 2
    rows, columns = part.shape
    part = part.reshape(2, n, rows // (2 * n), columns)
    piece = part.shape[1:]
    width = gain.shape[1] + extra.shape[1]
    dma = pltpu.SemaphoreType.DMA
    out, small = pl.pallas_call(
        functools.partial(total_kernel, dp, neg),
        out_shape=[
            jax.ShapeDtypeStruct(part.shape, part.dtype),
            jax.ShapeDtypeStruct((1, width), jnp.float32),
        ],
        in_specs=[VMEM] * 3,
        out_specs=[VMEM] * 2,
        scratch_shapes=[
            pltpu.VMEM(piece, part.dtype),
            pltpu.VMEM(piece, part.dtype),
            pltpu.VMEM(piece, part.dtype),
            pltpu.VMEM((1, width), jnp.float32),
            pltpu.VMEM((1, width), jnp.float32),
            pltpu.VMEM((n, 1, width), jnp.float32),
        ]
        + [dma((n,))] * 10
        + [dma] * 2,
        compiler_params=pltpu.CompilerParams(collective_id=ident, has_side_effects=True),
    )(part, gain, extra)
    return out.reshape(rows, columns), small


def select_tokens(rows, queries, per):
    token = lax.broadcasted_iota(jnp.int32, (rows, queries), 0)
    query = lax.broadcasted_iota(jnp.int32, (rows, queries), 1)
    return jnp.where(token // per == query, 1.0, 0.0)


def masked(passage, queries, length):
    scores = lax.dot_general(
        passage, queries, (((1,), (1,)), ((), ())), preferred_element_type=jnp.float32
    )
    position = lax.broadcasted_iota(jnp.int32, scores.shape, 0)
    return jnp.where(position < length, scores, LOW)


def forward_kernel(per, queries, passages, lengths, inner, similar):
    slots = passages.shape[0]
    tokens = queries.shape[0]
    inner[...] = jnp.zeros_like(inner)
    wide = tokens // 4 if tokens % 512 == 0 else tokens

    def one(p, carry):
        length = lengths[p, 0:1, 0:1]
        for start in range(0, tokens, wide):
            scores = masked(passages[p], queries[start : start + wide, :], length)
            highest = jnp.max(scores, axis=0, keepdims=True)
            lse = highest + jnp.log(jnp.sum(jnp.exp(scores - highest), axis=0, keepdims=True))
            inner[pl.ds(p, 1), start : start + wide] = lse
        return carry

    lax.fori_loop(0, slots, one, 0)
    chosen = select_tokens(tokens, similar.shape[1], per)
    summed = jnp.dot(
        inner[...], chosen, precision=lax.Precision.HIGHEST, preferred_element_type=jnp.float32
    )
    similar[...] = jnp.full_like(similar, LOW)
    for p in range(slots):
        shift = jnp.log(lengths[p, 0:1, 0:1].astype(jnp.float32)) * per
        similar[p : p + 1, :] = summed[p : p + 1, :] - shift


def backward_kernel(per, own, queries, passages, lengths, positives, inner, similar, everyone,
                    query_part, passage_part, loss_row, spread_coef, running):
    slots = passages.shape[0]
    tokens = queries.shape[0]
    neg = everyone.shape[0]
    here = lax.axis_index("neg")
    positive = positives[0]
    for s in range(1, neg):
        positive = positive + positives[s]
    positive = positive[0:1, :]
    highest = jnp.max(jnp.max(everyone[...], axis=0), axis=0, keepdims=True)
    row = lax.broadcasted_iota(jnp.int32, similar.shape, 0)
    exp_total = jnp.zeros(similar.shape, jnp.float32)
    score = jnp.zeros(similar.shape, jnp.float32)
    for s in range(neg):
        exp_total = exp_total + jnp.exp(everyone[s] - highest)
        score = score + jnp.where((row * neg + s == positive) & (row < slots), everyone[s], 0.0)
    log_total = highest + jnp.log(jnp.sum(exp_total, axis=0, keepdims=True))
    score = jnp.sum(score, axis=0, keepdims=True)
    lane = lax.broadcasted_iota(jnp.int32, log_total.shape, 1)
    mine = (lane >= here * own) & (lane < here * own + own)
    loss_row[...] = jnp.where(mine, log_total - score, 0.0)
    hit = jnp.where((row * neg + here == positive) & (row < slots), 1.0, 0.0)
    used = (row < slots) & (lax.broadcasted_iota(jnp.int32, similar.shape, 1) < tokens // per)
    coefficient = jnp.where(used, jnp.exp(similar[...] - log_total) - hit, 0.0)
    chosen = select_tokens(tokens, similar.shape[1], per)
    spread_coef[...] = lax.dot_general(
        coefficient, chosen, (((1,), (1,)), ((), ())),
        precision=lax.Precision.HIGHEST, preferred_element_type=jnp.float32,
    )
    running[...] = jnp.zeros_like(running)
    wide = tokens // 4 if tokens % 512 == 0 else tokens

    def one(p, carry):
        length = lengths[p, 0:1, 0:1]
        passage = passages[p]
        flipped = passage.astype(jnp.float32).T.astype(passage.dtype)
        total = jnp.zeros(passage.shape, jnp.float32)
        for start in range(0, tokens, wide):
            block = queries[start : start + wide, :]
            scores = masked(passage, block, length)
            spread = jnp.exp(scores - inner[pl.ds(p, 1), start : start + wide])
            weight = (spread * spread_coef[pl.ds(p, 1), start : start + wide]).astype(jnp.bfloat16)
            running[:, start : start + wide] += jnp.dot(
                flipped, weight, preferred_element_type=jnp.float32
            )
            total = total + jnp.dot(weight, block, preferred_element_type=jnp.float32)
        passage_part[p] = total.astype(passage_part.dtype)
        return carry

    lax.fori_loop(0, slots, one, 0)
    query_part[...] = running[...].T.astype(query_part.dtype)


def window_rows(resid_rows, context_rows, grad_rows, out_proj, norm_gain, colbert_proj):
    hidden = resid_rows.astype(jnp.float32) + jnp.dot(
        context_rows, out_proj, preferred_element_type=jnp.float32
    )
    row_mean = jnp.mean(hidden, axis=1, keepdims=True)
    centred = hidden - row_mean
    variance = jnp.mean(centred * centred, axis=1, keepdims=True)
    inv_std = 1.0 / jnp.sqrt(variance + 1e-05)
    normed = centred * inv_std
    scaled = (normed * norm_gain).astype(jnp.bfloat16)
    colbert_part = jnp.dot(scaled.T, grad_rows, preferred_element_type=jnp.float32)
    scaled_grad = jnp.dot(grad_rows, colbert_proj.T, preferred_element_type=jnp.float32)
    gain_part = jnp.sum(scaled_grad * normed, axis=0)
    gained = scaled_grad * norm_gain
    hidden_grad = (
        inv_std
        * (
            gained
            - jnp.mean(gained, axis=1, keepdims=True)
            - normed * jnp.mean(gained * normed, axis=1, keepdims=True)
        )
    ).astype(jnp.bfloat16)
    context_grad = jnp.dot(hidden_grad, out_proj.T, preferred_element_type=jnp.float32).astype(
        jnp.bfloat16
    )
    proj_part = jnp.dot(context_rows.T, hidden_grad, preferred_element_type=jnp.float32)
    return (hidden_grad, context_grad, proj_part, colbert_part, gain_part)


def body(sizes, query_emb, positive, passage_emb, lengths, residual, context, out_proj, norm_gain, colbert_proj):
    dp, neg = sizes["dp"], sizes["neg"]
    own, per, dim = query_emb.shape
    slots, plen = dp * passage_emb.shape[0], passage_emb.shape[1]
    group = own * neg
    tokens = group * per
    lanes = -(-group // LANES) * LANES
    rows = -(-slots // 8) * 8
    here = lax.axis_index("neg")
    pos_row = lax.dynamic_update_slice(jnp.zeros((8, lanes), jnp.int32), jnp.broadcast_to(positive, (8, own)), (0, here * own))
    len_row = jnp.broadcast_to(lengths, (8, LANES))
    queries, positives, passages, lens = gather(
        sizes,
        1,
        [
            (query_emb.reshape(own * per, dim), "neg"),
            (pos_row, "neg"),
            (passage_emb.reshape(plen, dim), "dp"),
            (len_row, "dp"),
        ],
    )
    queries = queries.reshape(tokens, dim)
    inner, similar = pl.pallas_call(
        functools.partial(forward_kernel, per),
        out_shape=[
            jax.ShapeDtypeStruct((rows, tokens), jnp.float32),
            jax.ShapeDtypeStruct((rows, lanes), jnp.float32),
        ],
        in_specs=[VMEM] * 3,
        out_specs=[VMEM] * 2,
    )(queries, passages, lens)
    (everyone,) = gather(sizes, 2, [(similar, "neg")])
    query_part, passage_part, loss_row = pl.pallas_call(
        functools.partial(backward_kernel, per, own),
        out_shape=[
            jax.ShapeDtypeStruct((tokens, dim), jnp.bfloat16),
            jax.ShapeDtypeStruct((slots, plen, dim), jnp.bfloat16),
            jax.ShapeDtypeStruct((1, lanes), jnp.float32),
        ],
        in_specs=[VMEM] * 7,
        out_specs=[VMEM] * 3,
        scratch_shapes=[pltpu.VMEM((rows, tokens), jnp.float32), pltpu.VMEM((dim, tokens), jnp.float32)],
    )(queries, passages, lens, positives, inner, similar, everyone)
    query_grad, emb_grad = scatter(
        sizes,
        3,
        [
            (query_part.reshape(neg, own * per, dim), "neg", jnp.float32),
            (passage_part, "dp", jnp.bfloat16),
        ],
    )
    residual_grad, context_grad, proj_part, colbert_part, gain_part = window_rows(
        residual, context, emb_grad, out_proj, norm_gain, colbert_proj
    )
    part = jnp.concatenate([proj_part.astype(jnp.bfloat16), colbert_part.astype(jnp.bfloat16)], axis=1)
    summed, small = total_sum(sizes, 4, part, gain_part[None, :], loss_row)
    width = norm_gain.shape[0]
    loss = jnp.sum(small[0, width:]) / (own * dp * neg)
    return (
        loss,
        query_grad.reshape(own, per, dim),
        residual_grad,
        context_grad,
        summed[:, :width].astype(jnp.float32),
        summed[:, width:].astype(jnp.float32),
        small[0, :width],
    )


def solution(mesh):
    sizes = {axis: mesh.shape[axis] for axis in ("dp", "neg")}
    split = ("dp", "neg")
    in_specs = (
        P(split, None, None),
        P(split),
        P(split, None, None),
        P(split),
        P(split, None),
        P(split, None),
        P(),
        P(),
        P(),
    )
    out_specs = (
        P(),
        P(split, None, None),
        P(split, None),
        P(split, None),
        P(),
        P(),
        P(),
    )
    return jax.shard_map(
        functools.partial(body, sizes), mesh=mesh, in_specs=in_specs, out_specs=out_specs, check_vma=False
    )
```

time: 306 us -> 151 us (0.49); the launches traced: 300 us -> 150 us
  Pallas kernels: 0 us -> 122 us
  waiting for transfers between devices: 119 us -> 0 us
  blocking collectives: 92.3 us -> 0 us
  matrix products: 38 us -> 8 us
  between operations: 19.5 us -> 3.23 us
  local copies, waits for them, and re-layouts: 18.2 us -> 8.38 us
  loops' own time: 3.08 us -> 0 us
    pallas_call x0 -> x6, Pallas kernels: none -> 122 us  [the longest x1 68.9 us: total_sum(): pl.pallas_call(functools.partial(total_kernel, dp, neg), out_shape=[jax.S...]
    psum x1 -> x0, waiting for transfers between devices: 98.7 us -> none  [body(): lax.psum((proj_part, colbert_part, gain_part, loss_part), ('dp', 'neg'))]
    psum x1 -> x0, blocking collectives: 40.7 us -> none  [body(): lax.psum((proj_part, colbert_part, gain_part, loss_part), ('dp', 'neg'))]
    all_gather x2 -> x0, blocking collectives: 29.1 us -> none  [the longest x1 15.4 us: body(): lax.all_gather(passage_emb, 'dp', axis=0, tiled=True)]
    dot_general x16 -> x0, matrix products: 25.3 us -> none  [the longest x8 11.3 us: masked_scores(): jnp.einsum('rd,jd->rj', query_block, passage_one, preferred_element_type=...]
    unnamed x3 -> x0, blocking collectives: 22.5 us -> none
    reduce_scatter x2 -> x0, waiting for transfers between devices: 19.9 us -> none  [the longest x1 19.9 us: body(): lax.psum_scatter(passage_sum, 'dp', scatter_dimension=0, tiled=True)]
    unnamed x36 -> x21, local copies, waits for them, and re-layouts: 11.6 us -> 1.91 us
  transfers between devices with their start and end apart: 3 -> 0, of which waited for: 2 -> 0; matrix products, arithmetic and copies ran while one was open for 4% -> 0% of each run, Pallas kernels for 0% -> 0%
where the time goes in v1:
time: 151 us; the launch traced here: 150 us
  Pallas kernels  122 us (81%)
  other arithmetic  9.03 us (6%)
  local copies, waits for them, and re-layouts  8.38 us (6%)
  matrix products  8 us (5%)
  between operations  3.23 us (2%)
    pallas_call x1, Pallas kernels, total_sum(): pl.pallas_call(functools.partial(total_kernel, dp, neg), out_shape=[jax.S...  68.9 us
    pallas_call x2, Pallas kernels, gather(): pl.pallas_call(functools.partial(gather_kernel, sizes, plan), out_shape=[...  23.5 us
    pallas_call x1, Pallas kernels, scatter(): pl.pallas_call(functools.partial(scatter_kernel, sizes, plan), out_shape=...  16 us
    pallas_call x1, Pallas kernels, body(): pl.pallas_call(functools.partial(backward_kernel, per, own), out_shape=[j...  7.92 us
    pallas_call x1, Pallas kernels, body(): pl.pallas_call(functools.partial(forward_kernel, per), out_shape=[jax.Sha...  5.16 us
    concatenate x1, local copies, waits for them, and re-layouts, body(): jnp.concatenate([proj_part.astype(jnp.bfloat16), colbert_part.astype(jnp....  4.31 us
    convert_element_type x1, other arithmetic, body(): summed[:, :width].astype(jnp.float32)  4.07 us

profile of v1, /device:TPU:29, one launch (start us, length us, event | category | flops | bytes accessed | tf_op | source)
XLA Modules:
  0.0 150.2 jit_solution(1795618992337318139)
XLA Ops:
  0.6 0.0 copy-start
  0.6 0.0 copy-start.8
  0.7 0.8 broadcast_in_dim.9
  1.5 0.2 dynamic_update_slice.3.refs_1_
  2.3 0.6 broadcast_in_dim.10.refs_3_
  2.9 0.0 copy-done.6
  2.9 16.3 %shard_map.147 = (bf16[8,128,128]{2,1,0:T(8,128)(2,1)}, s32[8,8,128]{2,1,0:T(8,128)}, bf16[4,512,128]{2,1,0:T(8,128)(2,1)}, s32[4,8,128]{2,1,0:T(8,128)}) custom-call(bf16[128,128]{1,0:T(8,128)(2,1)} %bitcast.30, s32[8,128]{1,0:T(8,128)} %copy-done.6, bf16[512,128]{1,0:T(8,128)(2,1)} %bitcast.28, s32[8,128]{1,0:T(8,128)} %broadcast_in_dim.10.refs_3_), custom_call_target="tpu_custom_call" | custom-call | tf_op jit(solution)/shard_map/pallas_call | solution.py:86
  19.2 5.2 %shard_map.148 = (f32[8,1024]{1,0:T(8,128)}, f32[8,128]{1,0:T(8,128)}) custom-call(bf16[1024,128]{1,0:T(8,128)(2,1)} %bitcast.25, bf16[4,512,128]{2,1,0:T(8,128)(2,1)} %get-tuple-element.21.passages, s32[4,8,128]{2,1,0:T(8,128)} %get-tuple-element.22.lengths), custom_call_target="tpu_custom_call" | custom-call | tf_op jit(solution)/shard_map/pallas_call | solution.py:432
  24.4 7.2 %shard_map.149.everyone = f32[8,8,128]{2,1,0:T(8,128)} custom-call(f32[8,128]{1,0:T(8,128)} %get-tuple-element.25.refs_0_.similar), custom_call_target="tpu_custom_call" | custom-call | tf_op jit(solution)/shard_map/pallas_call | solution.py:86
  31.6 7.9 %shard_map.150 = (bf16[1024,128]{1,0:T(8,128)(2,1)}, bf16[4,512,128]{2,1,0:T(8,128)(2,1)}, f32[1,128]{1,0:T(1,128)}) custom-call(bf16[1024,128]{1,0:T(8,128)(2,1)} %bitcast.26, bf16[4,512,128]{2,1,0:T(8,128)(2,1)} %get-tuple-element.21.passages, s32[4,8,128]{2,1,0:T(8,128)} %get-tuple-element.22.lengths, s32[8,8,128]{2,1,0:T(8,128)} %get-tuple-element.23.positives, ...), custom_call_target="tpu_custom_call" | custom-call | tf_op jit(solution)/shard_map/pallas_call | solution.py:442
  39.5 16.0 %shard_map.151 = (f32[128,128]{1,0:T(8,128)}, bf16[512,128]{1,0:T(8,128)(2,1)}) custom-call(bf16[8,128,128]{2,1,0:T(8,128)(2,1)} %bitcast.27, bf16[4,512,128]{2,1,0:T(8,128)(2,1)} %get-tuple-element.27.refs_1_), custom_call_target="tpu_custom_call" | custom-call | tf_op jit(solution)/shard_map/pallas_call | solution.py:145
  55.6 2.6 %fusion.3 = (f32[512]{0:T(512)S(1)}, f32[512,1024]{1,0:T(8,128)S(1)}) fusion(bf16[512,1024]{1,0:T(8,128)(2,1)} %param.14, bf16[1024,1024]{1,0:T(8,128)(2,1)S(1)} %copy-done, bf16[512,1024]{1,0:T(8,128)(2,1)S(1)} %copy-done.8), kind=kOutput, calls=%fused_computation.22 | convolution fusion | flops 1075314176 | bytes 6293504 | tf_op jit(solution)/shard_map/dot_general | solution.py:382
  58.2 0.0 copy-start.3
  58.2 0.0 copy-start.5
  58.2 0.3 multiply_reduce_fusion.2
  58.6 0.5 copy-done.2
  59.1 0.1 copy-done.3
  59.2 1.4 multiply_reduce_fusion
  60.6 0.6 multiply_convert_fusion.1
  61.2 0.6 copy-done.9
  61.8 1.3 convert_bitcast_fusion
  63.1 0.5 convolution_convert_fusion.1
  63.6 1.6 %pad_maximum_fusion = bf16[1024,1152]{0,1:T(8,128)(2,1)} fusion(bf16[1024,128]{0,1:T(8,128)(2,1)S(1)} %convolution_convert_fusion.1, bf16[1024,1024]{0,1:T(8,128)(2,1)S(1)} %convert_bitcast_fusion), kind=kLoop, calls=%fused_computation | loop fusion | flops 4718592 | bytes 4718592 | tf_op jit(solution)/shard_map/concatenate | solution.py:464
  65.2 4.3 %copy.16 = bf16[1024,1152]{1,0:T(8,128)(2,1)} copy(bf16[1024,1152]{0,1:T(8,128)(2,1)} %pad_maximum_fusion) | data formatting | bytes 4718592 | tf_op jit(solution)/shard_map/concatenate | solution.py:464
  69.6 68.9 %shard_map.152 = (bf16[2,16,32,1152]{3,2,1,0:T(8,128)(2,1)}, f32[1,1152]{1,0:T(1,128)}) custom-call(bf16[2,16,32,1152]{3,2,1,0:T(8,128)(2,1)} %bitcast.22, f32[1,1024]{1,0:T(1,128)} %bitcast.31, f32[1,128]{1,0:T(1,128)} %get-tuple-element.29.extra), custom_call_target="tpu_custom_call" | custom-call | tf_op jit(solution)/shard_map/pallas_call | solution.py:264
  138.5 4.1 %slice_convert_fusion = f32[1024,1024]{1,0:T(8,128)} fusion(bf16[1024,1152]{1,0:T(8,128)(2,1)} %bitcast.23), kind=kLoop, calls=%fused_computation.1 | loop fusion | flops 1048576 | bytes 6291456 | tf_op jit(solution)/shard_map/convert_element_type | solution.py:473
  142.5 1.8 %slice_convert_fusion.1 = f32[1024,128]{1,0:T(8,128)} fusion(bf16[1024,1152]{1,0:T(8,128)(2,1)} %bitcast.24), kind=kLoop, calls=%fused_computation.16 | loop fusion | flops 131072 | bytes 786432 | tf_op jit(solution)/shard_map/convert_element_type | solution.py:474
  144.3 0.0 copy-done.7
  144.3 0.6 slice.15
  144.9 0.6 slice_reduce_fusion
  146.2 2.3 %convolution_convert_fusion = bf16[512,1024]{1,0:T(8,128)(2,1)} fusion(bf16[512,1024]{1,0:T(8,128)(2,1)S(1)} %multiply_convert_fusion.1, bf16[1024,1024]{1,0:T(8,128)(2,1)S(1)} %copy-done), kind=kOutput, calls=%fused_computation.11 | convolution fusion | flops 1074266112 | bytes 4194304 | tf_op jit(solution)/shard_map/dot_general | solution.py:403
  148.5 0.6 copy.20
  (15 shorter events, 0.0 us)
Async XLA Ops:
  0.6 55.0 %copy-start = (bf16[1024,1024]{1,0:T(8,128)(2,1)S(1)}, bf16[1024,1024]{1,0:T(8,128)(2,1)}, u32[]{:S(2)}) copy-start(bf16[1024,1024]{1,0:T(8,128)(2,1)} %param.15) | copy-start | bytes 6291460
  0.6 55.0 %copy-start.8 = (bf16[512,1024]{1,0:T(8,128)(2,1)S(1)}, bf16[512,1024]{1,0:T(8,128)(2,1)}, u32[]{:S(2)}) copy-start(bf16[512,1024]{1,0:T(8,128)(2,1)} %param.13) | copy-start | bytes 3145732
  1.6 1.3 copy-start.6
  58.2 0.9 copy-start.2
  58.2 1.0 copy-start.3
  58.2 1.0 copy-start.5
  60.6 1.2 copy-start.9
  61.8 84.4 %copy-start.1 = (bf16[512,1024]{1,0:T(8,128)(2,1)}, bf16[512,1024]{1,0:T(8,128)(2,1)S(1)}, u32[]{:S(2)}) copy-start(bf16[512,1024]{1,0:T(8,128)(2,1)S(1)} %multiply_convert_fusion.1) | copy-start | bytes 3145732
  138.5 5.9 %copy-start.7 = (f32[1,1152]{1,0:T(1,128)S(1)}, f32[1,1152]{1,0:T(1,128)}, u32[]{:S(2)}) copy-start(f32[1,1152]{1,0:T(1,128)} %get-tuple-element.30) | copy-start | bytes 13828
  146.2 2.3 %copy-start.4 = (f32[128,128]{1,0:T(8,128)S(1)}, f32[128,128]{1,0:T(8,128)}, u32[]{:S(2)}) copy-start(f32[128,128]{1,0:T(8,128)} %get-tuple-element.31) | copy-start | bytes 196612
